TPU v7x, 32 devices: a whole 2x2x4 slice. The times are simulated.
32 devices in a mesh: dp: 8 (over z, x), tensor: 4 (over y, core).
Axes of the slice: x: 2, y: 2, z: 4, core: 2. Of those that a mesh axis runs over, the one named last changes fastest.
Arguments:
- tokens: bfloat16 [2048, 8192], P('dp', 'tensor'), may hold values from -6 to 6
- block_routing: int32 [8, 2], replicated, may hold values from -1 to 7, as said below
- frozen_up_weight: bfloat16 [8192, 28672], P('tensor', 'dp'), may hold values from -0.0625 to 0.0625
- adapter_down_weight: bfloat16 [32, 8192], P(None, 'tensor'), may hold values from -0.0625 to 0.0625
- adapter_up_weight: bfloat16 [32, 28672], P(None, 'dp'), may hold values from -6 to 6
- magnitude: float32 [28672], P('dp'), may hold values from 0.5 to 2
- cotangent: bfloat16 [1024, 28672], P('tensor', 'dp'), may hold values from -6 to 6
Outputs:
- projected: bfloat16 [1024, 28672], P('tensor', 'dp')
- grad_a: float32 [32, 8192], P(None, 'tensor')
- grad_b: float32 [32, 28672], P(None, 'dp')
- grad_m: float32 [28672], P('dp')
Inputs may be any that keep to these rules, and one draw needn't show every extreme that they name: `block_routing`: row d lists where the two blocks of dp index d go. Live blocks come first and -1 marks a padding block. A first live block stays on its own index; a second live block goes to index (d + half the dp size) mod the dp size, which then has no live block. Every dp index receives exactly one block. In every draw some index has two live blocks and some has none.
All inputs are finite; a program needn't handle non-finite values.
Results may differ from a plain program's by a relative error of at most 0.018.
Values may be sent and summed in bfloat16 or wider, within the bound.
A program may use at most 128 MiB of HBM per device.

v0:
```python
import math

import jax
import jax.numpy as jnp
from jax import lax
from jax.sharding import PartitionSpec as P

ADAPTER_RANK = 32
BLK = 128


def passed_along(value, axis, steps):
    count = lax.axis_size(axis)
    pairs = [(source, (source + steps) % count) for source in range(count)]
    return lax.ppermute(value, axis, pairs)


def contract_dims(left, right, left_dim, right_dim):
    return lax.dot_general(
        left, right, (((left_dim,), (right_dim,)), ((), ())), preferred_element_type=jnp.float32
    )


def body(
    tokens,
    block_routing,
    frozen_up_weight,
    adapter_down_weight,
    adapter_up_weight,
    magnitude,
    cotangent,
):
    dp_count = lax.axis_size("dp")
    tp_count = lax.axis_size("tensor")
    dp_index = lax.axis_index("dp")
    tp_index = lax.axis_index("tensor")
    adapter_scale = 1.0 / math.sqrt(ADAPTER_RANK)
    live_count = dp_count * BLK
    mine_count = live_count // tp_count
    own_row = lax.dynamic_index_in_dim(block_routing, dp_index, 0, keepdims=False)
    arrived = passed_along(tokens[BLK : 2 * BLK], "dp", dp_count // 2)
    own_block = jnp.where(own_row[0] == dp_index, tokens[:BLK], arrived)
    active_tokens = lax.all_gather(own_block, "dp", axis=0, tiled=True)
    rank_update = contract_dims(adapter_down_weight, adapter_up_weight, 0, 0)
    merged_weight = frozen_up_weight.astype(jnp.float32) + adapter_scale * rank_update
    col_part = jnp.sum(merged_weight * merged_weight, axis=0)
    down_factor_piece = contract_dims(active_tokens, adapter_down_weight, 1, 1)
    col_square, down_proj = (
        lax.psum(col_part.astype(jnp.bfloat16), "tensor").astype(jnp.float32),
        lax.psum(down_factor_piece.astype(jnp.bfloat16), "tensor").astype(jnp.float32),
    )
    col_norm = jnp.maximum(jnp.sqrt(col_square), 0.5)
    frozen_sum = lax.psum_scatter(
        jnp.dot(active_tokens, frozen_up_weight, preferred_element_type=jnp.float32).astype(
            jnp.bfloat16
        ),
        "tensor",
        scatter_dimension=0,
        tiled=True,
    ).astype(jnp.float32)
    row_start = tp_index * mine_count
    down_factor_half = lax.dynamic_slice_in_dim(down_proj, row_start, mine_count, 0).astype(
        jnp.bfloat16
    )
    unscaled_output = frozen_sum + adapter_scale * jnp.dot(
        down_factor_half, adapter_up_weight, preferred_element_type=jnp.float32
    )
    col_factor = magnitude / col_norm
    projected = (unscaled_output * col_factor).astype(jnp.bfloat16)
    inverse = 1.0 / math.sqrt(live_count)
    cot_full = cotangent.astype(jnp.float32)
    scaled_gradient = (cot_full * col_factor * inverse).astype(jnp.bfloat16)
    magnitude_part = jnp.sum(cot_full * unscaled_output, axis=0) / col_norm * inverse
    factor_part = adapter_scale * contract_dims(down_factor_half, scaled_gradient, 0, 0)
    grad_m, grad_b = (
        lax.psum(magnitude_part.astype(jnp.bfloat16), "tensor").astype(jnp.float32),
        lax.psum(factor_part.astype(jnp.bfloat16), "tensor").astype(jnp.float32),
    )
    row_piece = contract_dims(scaled_gradient, adapter_up_weight, 1, 1)
    summed = lax.psum(row_piece.astype(jnp.bfloat16), "dp")
    row_gradient = lax.all_gather(summed, "tensor", axis=0, tiled=True)
    grad_a = adapter_scale * contract_dims(row_gradient, active_tokens, 0, 0)
    return (projected, grad_a, grad_b, grad_m)


def solution(mesh):
    return jax.shard_map(
        body,
        mesh=mesh,
        in_specs=(
            P("dp", "tensor"),
            P(),
            P("tensor", "dp"),
            P(None, "tensor"),
            P(None, "dp"),
            P("dp"),
            P("tensor", "dp"),
        ),
        out_specs=(P("tensor", "dp"), P(None, "tensor"), P(None, "dp"), P("dp")),
        check_vma=False,
    )
```

profile of v0, /device:TPU:0, one launch (start us, length us, event | category | flops | bytes accessed | tf_op | source)
XLA Modules:
  0.0 268.7 jit_solution(4183278645062362374)
XLA Ops:
  7.2 0.0 copy-start
  7.2 0.0 all-gather.2.cloned.1.call-start
  7.2 1.1 slice.12
  8.4 4.1 %collective-permute-start = (bf16[128,2048]{1,0:T(8,128)(2,1)S(1)}, bf16[128,2048]{1,0:T(8,128)(2,1)S(1)}, u32[]{:S(2)}, u32[]{:S(2)}) collective-permute-start(bf16[128,2048]{1,0:T(8,128)(2,1)S(1)} %slice.12), channel_id=1, source_target_pairs={{0,16},{4,20},{8,24},{12,28},{16,0},{20,4},{24,8},{28,12},{1,17},{... | collective-permute-start | bytes 1572872 | tf_op jit(solution)/shard_map/ppermute | solution.py:15
  12.5 0.7 constant_dynamic-slice_fusion
  13.2 0.5 slice.10
  14.4 21.2 %collective-permute-done = bf16[128,2048]{1,0:T(8,128)(2,1)S(1)} collective-permute-done((bf16[128,2048]{1,0:T(8,128)(2,1)S(1)}, bf16[128,2048]{1,0:T(8,128)(2,1)S(1)}, u32[]{:S(2)}, u32[]{:S(2)}) %collective-permute-start) | collective-permute-done | bytes 524320 | tf_op jit(solution)/shard_map/ppermute | solution.py:15
  35.7 1.9 slice_select_fusion
  37.5 0.0 all-gather.2.cloned.1.call-update
  37.6 0.0 all-reduce.3.cloned.1.call-start
  37.6 10.3 %multiply_reduce_fusion = bf16[3584]{0:T(1024)(128)(2,1)S(1)} fusion(bf16[2048,3584]{1,0:T(8,128)(2,1)} %param.9, bf16[32,2048]{1,0:T(8,128)(2,1)} %param.10, bf16[32,3584]{1,0:T(8,128)(2,1)S(1)} %copy-done), kind=kOutput, calls=%fused_computation | convolution fusion | flops 506458624 | bytes 15047680 | tf_op jit(solution)/shard_map/dot_general | solution.py:19
  48.0 6.5 %psum.36 = bf16[3584]{0:T(1024)(128)(2,1)S(1)} all-reduce(bf16[3584]{0:T(1024)(128)(2,1)S(1)} %multiply_reduce_fusion), channel_id=1, replica_groups=mesh['dp'=8,'tensor'=4] {'tensor'}, use_global_device_ids=true, to_apply=%region_3.4 | all-reduce | flops 3584 | bytes 14336 | tf_op jit(solution)/shard_map/psum | solution.py:49
  54.5 57.2 %all-gather.2.cloned.1.call-done = bf16[1024,2048]{1,0:T(8,128)(2,1)} async-done(((bf16[128,2048]{1,0:T(8,128)(2,1)}), bf16[1024,2048]{1,0:T(8,128)(2,1)}) %all-gather.2.cloned.1.call-update) | async-done | bytes 4194320 | tf_op jit(solution)/shard_map/all_gather | solution.py:43
  111.7 4.2 %convolution_convert_fusion.1 = bf16[1024,32]{0,1:T(8,128)(2,1)} fusion(bf16[1024,2048]{1,0:T(8,128)(2,1)} %all-gather.2.cloned.1.call-done, bf16[32,2048]{1,0:T(8,128)(2,1)S(1)} %copy-done.2), kind=kOutput, calls=%fused_computation.15 | convolution fusion | flops 134250496 | bytes 4390912 | tf_op jit(solution)/shard_map/dot_general | solution.py:19
  115.9 0.0 all-reduce.3.cloned.1.call-update
  115.9 0.0 all-reduce.5.cloned.1.call-start
  116.0 30.1 %all-reduce.3.cloned.1.call-done = bf16[1024,32]{0,1:T(8,128)(2,1)} async-done(((bf16[1024,32]{0,1:T(8,128)(2,1)}), bf16[1024,32]{0,1:T(8,128)(2,1)}) %all-reduce.3.cloned.1.call-update) | async-done | bytes 65552 | tf_op jit(solution)/shard_map/psum | solution.py:50
  146.1 2.0 fusion
  148.1 0.0 all-reduce.5.cloned.1.call-update
  148.2 0.0 reduce-scatter.2.cloned.1.call-start
  148.2 21.7 %convolution_convert_fusion = bf16[1024,3584]{1,0:T(8,128)(2,1)} fusion(bf16[1024,2048]{1,0:T(8,128)(2,1)} %all-gather.2.cloned.1.call-done, bf16[2048,3584]{1,0:T(8,128)(2,1)} %param.9), kind=kOutput, calls=%fused_computation.1 | convolution fusion | flops 15036055552 | bytes 26214400 | tf_op jit(solution)/shard_map/dot_general | solution.py:54
  170.0 0.0 reduce-scatter.2.cloned.1.call-update
  170.0 0.6 fusion.7
  170.6 37.5 %psum.37 = bf16[256,32]{1,0:T(8,128)(2,1)S(1)} all-reduce(bf16[256,32]{1,0:T(8,128)(2,1)S(1)} %fusion.7), channel_id=1, replica_groups=mesh['dp'=8,'tensor'=4] {'dp'}, use_global_device_ids=true, to_apply=%region_4.5 | all-reduce | flops 8192 | bytes 32768 | tf_op jit(solution)/shard_map/psum | solution.py:80
  208.2 7.5 %all_gather.7 = bf16[1024,32]{1,0:T(8,128)(2,1)S(1)} all-gather(bf16[256,32]{1,0:T(8,128)(2,1)S(1)} %psum.37), channel_id=1, replica_groups=mesh['dp'=8,'tensor'=4] {'tensor'}, dimensions={0}, use_global_device_ids=true | all-gather | bytes 81920 | tf_op jit(solution)/shard_map/all_gather | solution.py:81
  215.7 3.7 %convolution_multiply_fusion.2 = f32[32,2048]{1,0:T(8,128)} fusion(bf16[1024,32]{1,0:T(8,128)(2,1)S(1)} %all_gather.7, bf16[1024,2048]{1,0:T(8,128)(2,1)} %all-gather.2.cloned.1.call-done), kind=kOutput, calls=%fused_computation.12 | convolution fusion | flops 134283264 | bytes 4521984 | tf_op jit(solution)/shard_map/dot_general | solution.py:19
  219.5 3.3 %convolution_multiply_fusion = f32[256,3584]{1,0:T(8,128)} fusion(bf16[32,3584]{1,0:T(8,128)(2,1)S(1)} %copy-done, bf16[1024,32]{0,1:T(8,128)(2,1)} %all-reduce.3.cloned.1.call-done, s32[]{:T(128)S(6)} %select_n.18), kind=kOutput, calls=%fused_computation.2 | convolution fusion | flops 59654144 | bytes 3915780 | tf_op jit(solution)/shard_map/dot_general | solution.py:65
  222.7 1.7 convert_element_type.61
  224.5 26.5 %reduce-scatter.2.cloned.1.call-done = bf16[256,3584]{1,0:T(8,128)(2,1)} async-done(((bf16[1024,3584]{1,0:T(8,128)(2,1)}), bf16[256,3584]{1,0:T(8,128)(2,1)}) %reduce-scatter.2.cloned.1.call-update) | async-done | bytes 1835024 | tf_op jit(solution)/shard_map/reduce_scatter | solution.py:53
  251.0 4.6 %fusion.3 = (f32[3584]{0:T(1024)S(1)}, bf16[256,3584]{1,0:T(8,128)(2,1)}) fusion(bf16[256,3584]{1,0:T(8,128)(2,1)S(1)} %copy-done.1, f32[256,3584]{1,0:T(8,128)} %convolution_multiply_fusion, bf16[256,3584]{1,0:T(8,128)(2,1)} %reduce-scatter.2.cloned.1.call-done, f32[3584]{0:T(1024)S(1)} %fusion.10), kind=kLoop, calls=%fused_computation.9 | loop fusion | flops 6418944 | bytes 9203712 | tf_op jit(solution)/shard_map/reduce_sum | solution.py:73
  255.7 5.9 %psum.39 = bf16[3584]{0:T(1024)(128)(2,1)S(1)} all-reduce(bf16[3584]{0:T(1024)(128)(2,1)S(1)} %multiply_convert_fusion.1), channel_id=1, replica_groups=mesh['dp'=8,'tensor'=4] {'tensor'}, use_global_device_ids=true, to_apply=%region_7.8 | all-reduce | flops 3584 | bytes 14336 | tf_op jit(solution)/shard_map/psum | solution.py:76
  261.6 0.6 convert_element_type.63
  (10 shorter events, 0.1 us)
Async XLA Ops:
  7.2 30.5 %copy-start = (bf16[32,3584]{1,0:T(8,128)(2,1)S(1)}, bf16[32,3584]{1,0:T(8,128)(2,1)}, u32[]{:S(2)}) copy-start(bf16[32,3584]{1,0:T(8,128)(2,1)} %param.11) | copy-start | bytes 688132
  7.2 104.5 %all-gather.2.cloned.1.call-start = ((), (), s32[]{:S(2)}) async-start(), calls=%async_computation.1 | async-start | bytes 4718592 | tf_op jit(solution)/shard_map/all_gather | solution.py:43
  8.4 27.3 %collective-permute-start = (bf16[128,2048]{1,0:T(8,128)(2,1)S(1)}, bf16[128,2048]{1,0:T(8,128)(2,1)S(1)}, u32[]{:S(2)}, u32[]{:S(2)}) collective-permute-start(bf16[128,2048]{1,0:T(8,128)(2,1)S(1)} %slice.12), channel_id=1, source_target_pairs={{0,16},{4,20},{8,24},{12,28},{16,0},{20,4},{24,8},{28,12},{1,17},{... | collective-permute-start | bytes 1572872 | tf_op jit(solution)/shard_map/ppermute | solution.py:15
  37.6 74.1 %copy-start.2 = (bf16[32,2048]{1,0:T(8,128)(2,1)S(1)}, bf16[32,2048]{1,0:T(8,128)(2,1)}, u32[]{:S(2)}) copy-start(bf16[32,2048]{1,0:T(8,128)(2,1)} %param.10) | copy-start | bytes 393220
  37.6 108.5 %all-reduce.3.cloned.1.call-start = ((), (), s32[]{:S(2)}) async-start(), calls=%async_computation.3 | async-start | bytes 131072 | tf_op jit(solution)/shard_map/psum | solution.py:50
  48.0 68.0 %copy-start.3 = (f32[3584]{0:T(1024)S(1)}, f32[3584]{0:T(1024)}, u32[]{:S(2)}) copy-start(f32[3584]{0:T(1024)} %param.12) | copy-start | bytes 43012
  48.0 98.1 %copy-start.1 = (bf16[256,3584]{1,0:T(8,128)(2,1)S(1)}, bf16[256,3584]{1,0:T(8,128)(2,1)}, u32[]{:S(2)}) copy-start(bf16[256,3584]{1,0:T(8,128)(2,1)} %param.13) | copy-start | bytes 5505028
  115.9 106.9 %all-reduce.5.cloned.1.call-start = ((), (), s32[]{:S(2)}) async-start(), calls=%async_computation.4 | async-start | bytes 458752 | tf_op jit(solution)/shard_map/psum | solution.py:77
  148.2 102.8 %reduce-scatter.2.cloned.1.call-start = ((), (), s32[]{:S(2)}) async-start(), calls=%async_computation.2 | async-start | bytes 9175040 | tf_op jit(solution)/shard_map/reduce_scatter | solution.py:53
Sparse Core Ops, SparseCore 0:
  37.7 73.9 all-gather.1
  116.0 30.0 all-reduce.2
  149.0 32.1 all-reduce.4
  183.6 67.3 reduce-scatter.1
where the time goes:
time: 269 us
  waiting for transfers between devices  135 us (50%)
  blocking collectives  57.4 us (21%)
  matrix products  45.9 us (17%)
  between operations  14.5 us (5%)
  other arithmetic  8.91 us (3%)
  starting transfers between devices  4.29 us (2%)
    all_gather x1, waiting for transfers between devices, body(): active_tokens = lax.all_gather(own_block, 'dp', axis=0, tiled=True)  57.2 us
    psum x1, blocking collectives, body(): summed = lax.psum(row_piece.astype(jnp.bfloat16), 'dp')  37.5 us
    psum x1, waiting for transfers between devices, body(): lax.psum(down_factor_piece.astype(jnp.bfloat16), 'tensor')  30.1 us
    reduce_scatter x1, waiting for transfers between devices, body(): lax.psum_scatter(jnp.dot(active_tokens, frozen_up_weight, preferred_eleme...  26.5 us
    dot_general x1, matrix products, body(): jnp.dot(active_tokens, frozen_up_weight, preferred_element_type=jnp.float32)  21.7 us
    ppermute x1, waiting for transfers between devices, passed_along(): return lax.ppermute(value, axis, pairs)  21.2 us
    dot_general x5, matrix products, contract_dims(): lax.dot_general(left, right, (((left_dim,), (right_dim,)), ((), ())), pre...  20.9 us
    all_gather x1, blocking collectives, body(): row_gradient = lax.all_gather(summed, 'tensor', axis=0, tiled=True)  7.54 us
  transfers between devices with their start and end apart: 5, of which 4 were waited for; matrix products, arithmetic and copies ran while one was open for 16% of the time, Pallas kernels for 0%

commit v1 on v0

v1 whole, which is shorter than its diff:
```python
import functools
import math

import jax
import jax.numpy as jnp
from jax import lax
from jax.experimental import pallas as pl
from jax.experimental.pallas import tpu as pltpu
from jax.sharding import PartitionSpec as P

BLK = 128
ROWS = 16
CHUNKS = BLK // ROWS
AHEAD = 3
LANES = 128
MESH = pl.DeviceIdType.MESH
F32 = jnp.float32
BF16 = jnp.bfloat16


def mirrored(value, bits):
    result = 0
    for position in range(bits):
        result = result + (value // (1 << position)) % 2 * (1 << (bits - 1 - position))
    return result


def flipped(value, bit):
    return value + bit - 2 * bit * ((value // bit) % 2)


def dots(left, right, left_dim, right_dim):
    return lax.dot_general(
        left, right, (((left_dim,), (right_dim,)), ((), ())), preferred_element_type=F32
    )


def kernel(
    cfg,
    tok_in, routing, w_hbm, down, up, mag, cot,
    out, ga_out, gb_out, gm_out,
    w, raw, tok, part, near, pair, far, downp, sq, sq_near, sq_far, factor, norm, sg,
    rp, rp_in, rgt, rg, proj_down, gm_acc, gb_part, gb_near, gb_sum, gb_far, gm_part, gm_in,
    w_sem, s0_send, s0_recv, st_send, st_recv, nr_send, nr_recv, fr_send, fr_recv, ms_send, ms_recv,
):
    dp, tp, width, cols, rank, tile, tps = cfg
    bits = dp.bit_length() - 1
    per = dp // tp
    tiles = cols // tile
    scale = 1.0 / math.sqrt(rank)
    inverse = 1.0 / math.sqrt(dp * BLK)
    d = lax.axis_index("dp")
    t = lax.axis_index("tensor")
    core = t % 2
    side = t // 2
    t_near, t_far = flipped(t, 1), flipped(t, 2)
    hops = [flipped(d, dp >> (k + 1)) for k in range(bits)]

    def copy(src, dst, send, recv, target):
        return pltpu.make_async_remote_copy(
            src_ref=src, dst_ref=dst, send_sem=send, recv_sem=recv,
            device_id=target, device_id_type=MESH,
        )

    def to_dp(k):
        return {"dp": hops[k]}

    near_id, far_id = {"tensor": t_near}, {"tensor": t_far}

    def w_copy(n):
        at = pl.ds(pl.multiple_of(n * tile, tile), tile)
        return pltpu.make_async_copy(w_hbm.at[:, at], w.at[:, at], w_sem.at[n])

    def first(c):
        return copy(tok_in.at[:, c], raw.at[c], s0_send.at[c], s0_recv.at[c], to_dp(0))

    def stage(k, c, owner):
        size = 1 << k
        base = mirrored(owner, bits) // size * size
        here = tok.at[c, pl.ds(pl.multiple_of(base * ROWS, ROWS), size * ROWS)]
        return copy(here, here, st_send.at[k - 1, c], st_recv.at[k - 1, c], to_dp(k))

    def near_copy(c):
        start = (1 - core) * 2
        return copy(part.at[c, :, pl.ds(start, 2)], near.at[c], nr_send.at[c], nr_recv.at[c], near_id)

    def far_copy(c):
        return copy(pair.at[c], far.at[c], fr_send.at[c], fr_recv.at[c], far_id)

    def small(n, src, dst, target):
        return copy(src, dst, ms_send.at[n], ms_recv.at[n], target)

    sq1 = small(0, sq, sq_near, near_id)
    sq2 = small(1, sq_near, sq_far, far_id)
    rp_hops = [small(2 + k, rp.at[k], rp_in.at[k], to_dp(k)) for k in range(bits)]
    n0 = 2 + bits
    rg1 = small(n0, rgt.at[t], rgt.at[t], near_id)
    rg1_in = small(n0, rgt.at[t_near], rgt.at[t_near], near_id)
    mine2 = pl.ds(side * 2, 2)
    theirs2 = pl.ds((1 - side) * 2, 2)
    rg2 = small(n0 + 1, rgt.at[mine2], rgt.at[mine2], far_id)
    rg2_in = small(n0 + 1, rgt.at[theirs2], rgt.at[theirs2], far_id)

    def each_tile(body):
        @pl.loop(0, tiles)
        def _(n):
            body(pl.ds(pl.multiple_of(n * tile, tile), tile))

    @pl.loop(0, tiles)
    def _(n):
        w_copy(n).start()

    barrier = pltpu.get_barrier_semaphore()
    for k in range(bits):
        pl.semaphore_signal(barrier, inc=1, device_id=to_dp(k), device_id_type=MESH)
    pl.semaphore_signal(barrier, inc=1, device_id=near_id, device_id_type=MESH)
    pl.semaphore_signal(barrier, inc=1, device_id=far_id, device_id_type=MESH)
    pl.semaphore_wait(barrier, bits + 2)

    for c in range(AHEAD):
        first(c).start()
    downp[...] = jnp.zeros_like(downp)
    downp[:rank, :] = down[...]
    gm_acc[...] = jnp.zeros_like(gm_acc)

    own_live = routing[d, 0] == d
    pair_live = routing[hops[0], 0] == hops[0]
    norm_last = (tiles + tps - 1) // tps - 1
    depth = 256

    def norm_tile(n):
        w_copy(n).wait()
        at = pl.ds(pl.multiple_of(n * tile, tile), tile)

        def add(r, total):
            rows = pl.ds(pl.multiple_of(r * depth, depth), depth)
            merged = w[rows, at].astype(F32) + scale * dots(down[:, rows], up[:, at], 0, 0)
            return total + jnp.sum((merged * merged).reshape(depth // 8, 8, tile), axis=0)

        total = lax.fori_loop(0, width // depth, add, jnp.zeros((8, tile), F32))
        sq[:, at] = jnp.sum(total, axis=0, keepdims=True)

    def gradient():
        def body(at):
            square = sq_near[:, at] + sq_far[:, at]
            size = jnp.maximum(jnp.sqrt(square), 0.5)
            ratio = mag[:, at] / size
            norm[:, at] = size
            factor[:, at] = ratio
            for g in range(per):
                sg[g, :, at] = (cot[g, :, at].astype(F32) * ratio * inverse).astype(BF16)

        each_tile(body)
        for g in range(per):
            rp[0, :, g * BLK:(g + 1) * BLK] = dots(up[...], sg[g], 1, 1)
        rp_hops[0].start()

    def epilogue(c):
        mine = core * 2 + side
        rows = pl.ds(pl.multiple_of(c * ROWS, ROWS), ROWS)
        high = per * ROWS

        def total(at, wide):
            return (
                part[c, :, mine, :, at].astype(F32)
                + near[c, :, side, :, at].astype(F32)
                + far[c, :, :, at].astype(F32)
            ).reshape(high, wide)

        small_down = total(pl.ds(cols, LANES), LANES).astype(BF16)
        proj_down[:, rows, :] = small_down.reshape(per, ROWS, LANES)
        lhs = small_down[:, :rank]

        def body(at):
            pre = total(at, tile) + scale * jnp.dot(lhs, up[:, at], preferred_element_type=F32)
            out[:, rows, at] = (pre * factor[:, at]).astype(BF16).reshape(per, ROWS, tile)
            both = cot[:, rows, at].astype(F32).reshape(high, tile) * pre
            gm_acc[:, at] += jnp.sum(both.reshape(high // 8, 8, tile), axis=0)

        each_tile(body)

    def when(condition, action):
        pl.when(condition)(action)

    steps = CHUNKS + bits + 1

    @pl.loop(0, steps)
    def _(i):
        when(i + AHEAD < CHUNKS, lambda: first(i + AHEAD).start())

        @pl.when(i < CHUNKS)
        def _():
            first(i).wait_recv()
            own_at = pl.ds(pl.multiple_of(mirrored(d, bits) * ROWS, ROWS), ROWS)
            pair_at = pl.ds(pl.multiple_of(mirrored(hops[0], bits) * ROWS, ROWS), ROWS)
            tok[i, own_at] = jnp.where(own_live, tok_in[0, i], raw[i, 1])
            tok[i, pair_at] = jnp.where(pair_live, raw[i, 0], tok_in[1, i])
            stage(1, i, d).start()

        for k in range(1, bits):
            j = i - k

            @pl.when((j >= 0) & (j < CHUNKS))
            def _():
                stage(k, j, hops[k]).wait_recv()
                if k < bits - 1:
                    stage(k + 1, j, d).start()

        @pl.when(i <= norm_last)
        def _():
            for e in range(tps):
                n = i * tps + e
                when(n < tiles, lambda: norm_tile(n))

        when(i == norm_last, lambda: sq1.start())

        @pl.when(i == norm_last + 1)
        def _():
            sq1.wait()
            sq_near[...] = sq_near[...] + sq[...]
            sq2.start()

        @pl.when(i == norm_last + 2)
        def _():
            sq2.wait()
            gradient()

        for k in range(bits):
            @pl.when(i == norm_last + 3 + k)
            def _():
                rp_hops[k].wait()
                merged = rp[k] + rp_in[k]
                if k < bits - 1:
                    rp[k + 1] = merged
                    rp_hops[k + 1].start()
                else:
                    rgt[t] = merged.astype(BF16)
                    rg1.start()

        @pl.when(i == norm_last + 3 + bits)
        def _():
            rg1.wait_send()
            rg1_in.wait_recv()
            rg2.start()

        j_near = i - bits

        @pl.when((j_near >= 0) & (j_near < CHUNKS))
        def _():
            near_copy(j_near).wait_recv()
            other = core * 2 + 1 - side

            def body(at):
                pair[j_near, :, :, at] = (
                    part[j_near, :, other, :, at].astype(F32)
                    + near[j_near, :, 1 - side, :, at].astype(F32)
                ).astype(BF16)

            each_tile(body)
            body(pl.ds(cols, LANES))
            far_copy(j_near).start()

        j_mat = i - (bits - 1)

        @pl.when((j_mat >= 0) & (j_mat < CHUNKS))
        def _():
            lhs = tok.at[j_mat]

            def body(at):
                prod = jnp.dot(lhs[...], w[:, at], preferred_element_type=F32)
                part[j_mat, :, :, :, at] = prod.astype(BF16).reshape(per, tp, ROWS, tile)

            each_tile(body)
            part[j_mat, :, :, :, cols:] = (
                dots(lhs[...], downp[...], 1, 1).astype(BF16).reshape(per, tp, ROWS, LANES)
            )
            near_copy(j_mat).start()

        j_far = i - bits - 1

        @pl.when((j_far >= 0) & (j_far < CHUNKS - 1))
        def _():
            far_copy(j_far).wait_recv()
            epilogue(j_far)

    rg2.wait_send()
    rg2_in.wait_recv()
    for s in range(tp):
        turned = rgt[s].astype(F32).T.astype(BF16)
        spot = s % 2 * 2 + s // 2
        for g in range(per):
            for c in range(CHUNKS):
                low = g * BLK + c * ROWS
                rg[c, g, spot] = turned[low:low + ROWS]

    wide = min(512, width)

    @pl.loop(0, width // wide)
    def _(n):
        at = pl.ds(pl.multiple_of(n * wide, wide), wide)

        def add(c, total):
            return total + dots(rg[c].reshape(dp * ROWS, rank), tok[c, :, at], 0, 0)

        ga_out[:, at] = scale * lax.fori_loop(0, CHUNKS, add, jnp.zeros((rank, wide), F32))

    far_copy(CHUNKS - 1).wait_recv()
    epilogue(CHUNKS - 1)

    n1 = n0 + 2
    gb1 = small(n1, gb_part, gb_near, near_id)
    gb2 = small(n1 + 1, gb_sum, gb_far, far_id)
    gm1 = small(n1 + 2, gm_part.at[0], gm_in.at[0], near_id)
    gm2 = small(n1 + 3, gm_part.at[1], gm_in.at[1], far_id)
    live = proj_down[...].reshape(per * BLK, LANES)[:, :rank]

    def ends(at):
        gb_part[:, at] = (
            scale * dots(live, sg[:, :, at].reshape(per * BLK, tile), 0, 0)
        ).astype(BF16)
        gm_part[0, :, at] = (
            jnp.sum(gm_acc[:, at], axis=0, keepdims=True) / norm[:, at] * inverse
        )

    each_tile(ends)
    gm1.start()
    gb1.start()
    gm1.wait()
    gm_part[1] = gm_part[0] + gm_in[0]
    gm2.start()
    gb1.wait()

    def sums(at):
        gb_sum[:, at] = (gb_part[:, at].astype(F32) + gb_near[:, at].astype(F32)).astype(BF16)

    each_tile(sums)
    gb2.start()
    gm2.wait()
    gm_out[...] = gm_part[1] + gm_in[1]
    gb2.wait()

    def last(at):
        gb_out[:, at] = gb_sum[:, at].astype(F32) + gb_far[:, at].astype(F32)

    each_tile(last)

    @pl.loop(0, CHUNKS)
    def _(c):
        first(c).wait_send()
        for k in range(1, bits):
            stage(k, c, d).wait_send()
        near_copy(c).wait_send()
        far_copy(c).wait_send()


def body(dp, tp, tokens, routing, weight, down, up, mag, cot):
    width, cols = weight.shape
    rank = down.shape[0]
    per = dp // tp
    bits = dp.bit_length() - 1
    tile = next(size for size in (512, 256, 128) if cols % size == 0)
    tiles = cols // tile
    tps = -(-tiles // bits)
    cfg = (dp, tp, width, cols, rank, tile, tps)
    ext = cols + LANES
    vmem = pl.BlockSpec(memory_space=pltpu.VMEM)
    dma = pltpu.SemaphoreType.DMA
    mine = per * BLK
    misc = bits + 8
    out, ga, gb, gm = pl.pallas_call(
        functools.partial(kernel, cfg),
        out_shape=(
            jax.ShapeDtypeStruct((per, BLK, cols), BF16),
            jax.ShapeDtypeStruct((rank, width), F32),
            jax.ShapeDtypeStruct((rank, cols), F32),
            jax.ShapeDtypeStruct((1, cols), F32),
        ),
        in_specs=[
            vmem,
            pl.BlockSpec(memory_space=pltpu.SMEM),
            pl.BlockSpec(memory_space=pl.ANY),
            vmem, vmem, vmem, vmem,
        ],
        out_specs=(vmem, vmem, vmem, vmem),
        scratch_shapes=[
            pltpu.VMEM((width, cols), BF16),
            pltpu.VMEM((CHUNKS, 2, ROWS, width), BF16),
            pltpu.VMEM((CHUNKS, dp * ROWS, width), BF16),
            pltpu.VMEM((CHUNKS, per, tp, ROWS, ext), BF16),
            pltpu.VMEM((CHUNKS, per, 2, ROWS, ext), BF16),
            pltpu.VMEM((CHUNKS, per, ROWS, ext), BF16),
            pltpu.VMEM((CHUNKS, per, ROWS, ext), BF16),
            pltpu.VMEM((LANES, width), BF16),
            pltpu.VMEM((1, cols), F32),
            pltpu.VMEM((1, cols), F32),
            pltpu.VMEM((1, cols), F32),
            pltpu.VMEM((1, cols), F32),
            pltpu.VMEM((1, cols), F32),
            pltpu.VMEM((per, BLK, cols), BF16),
            pltpu.VMEM((bits, rank, mine), F32),
            pltpu.VMEM((bits, rank, mine), F32),
            pltpu.VMEM((tp, rank, mine), BF16),
            pltpu.VMEM((CHUNKS, per, tp, ROWS, rank), BF16),
            pltpu.VMEM((per, BLK, LANES), BF16),
            pltpu.VMEM((8, cols), F32),
            pltpu.VMEM((rank, cols), BF16),
            pltpu.VMEM((rank, cols), BF16),
            pltpu.VMEM((rank, cols), BF16),
            pltpu.VMEM((rank, cols), BF16),
            pltpu.VMEM((2, 1, cols), F32),
            pltpu.VMEM((2, 1, cols), F32),
            dma((tiles,)),
            dma((CHUNKS,)), dma((CHUNKS,)),
            dma((bits - 1, CHUNKS)), dma((bits - 1, CHUNKS)),
            dma((CHUNKS,)), dma((CHUNKS,)),
            dma((CHUNKS,)), dma((CHUNKS,)),
            dma((misc,)), dma((misc,)),
        ],
        compiler_params=pltpu.CompilerParams(
            collective_id=0, has_side_effects=True, vmem_limit_bytes=67043328
        ),
    )(
        tokens.reshape(2, CHUNKS, ROWS, width),
        routing,
        weight,
        down,
        up,
        mag.reshape(1, cols),
        cot.reshape(per, BLK, cols),
    )
    return out.reshape(mine, cols), ga, gb, gm.reshape(cols)


def solution(mesh):
    return jax.shard_map(
        functools.partial(body, mesh.shape["dp"], mesh.shape["tensor"]),
        mesh=mesh,
        in_specs=(
            P("dp", "tensor"),
            P(),
            P("tensor", "dp"),
            P(None, "tensor"),
            P(None, "dp"),
            P("dp"),
            P("tensor", "dp"),
        ),
        out_specs=(P("tensor", "dp"), P(None, "tensor"), P(None, "dp"), P("dp")),
        check_vma=False,
    )
```

time: 269 us -> 118 us (0.44)
  waiting for transfers between devices: 135 us -> 0 us
  Pallas kernels: 0 us -> 109 us
  blocking collectives: 57.4 us -> 0 us
  matrix products: 45.9 us -> 0 us
  between operations: 14.5 us -> 0.64 us
  other arithmetic: 8.91 us -> 1.36 us
  local copies, waits for them, and re-layouts: 2.43 us -> 7.06 us
  starting transfers between devices: 4.29 us -> 0 us
    pallas_call x0 -> x1, Pallas kernels: none -> 109 us  [body(): pl.pallas_call(functools.partial(kernel, cfg), out_shape=(jax.ShapeDtypeS...]
    all_gather x1 -> x0, waiting for transfers between devices: 57.2 us -> none  [body(): active_tokens = lax.all_gather(own_block, 'dp', axis=0, tiled=True)]
    psum x3 -> x0, blocking collectives: 49.9 us -> none  [the longest x1 37.5 us: body(): summed = lax.psum(row_piece.astype(jnp.bfloat16), 'dp')]
    dot_general x7 -> x0, matrix products: 45.9 us -> none  [the longest x1 21.7 us: body(): jnp.dot(active_tokens, frozen_up_weight, preferred_element_type=jnp.float32)]
    psum x2 -> x0, waiting for transfers between devices: 30.1 us -> none  [the longest x1 30.1 us: body(): lax.psum(down_factor_piece.astype(jnp.bfloat16), 'tensor')]
    reduce_scatter x1 -> x0, waiting for transfers between devices: 26.5 us -> none  [body(): lax.psum_scatter(jnp.dot(active_tokens, frozen_up_weight, preferred_eleme...]
    ppermute x1 -> x0, waiting for transfers between devices: 21.2 us -> none  [passed_along(): return lax.ppermute(value, axis, pairs)]
    all_gather x1 -> x0, blocking collectives: 7.54 us -> none  [body(): row_gradient = lax.all_gather(summed, 'tensor', axis=0, tiled=True)]
  transfers between devices with their start and end apart: 5 -> 0, of which waited for: 4 -> 0; matrix products, arithmetic and copies ran while one was open for 16% -> 0% of each run, Pallas kernels for 0% -> 0%
where the time goes in v1:
time: 118 us
  Pallas kernels  109 us (92%)
  local copies, waits for them, and re-layouts  7.06 us (6%)
  other arithmetic  1.36 us (1%)
    pallas_call x1, Pallas kernels, body(): pl.pallas_call(functools.partial(kernel, cfg), out_shape=(jax.ShapeDtypeS...  109 us
    unnamed x8, local copies, waits for them, and re-layouts  5.74 us

profile of v1, /device:TPU:0, one launch (start us, length us, event | category | flops | bytes accessed | tf_op | source)
XLA Modules:
  0.0 117.9 jit_solution(10314167750474538600)
XLA Ops:
  0.6 1.3 %copy.11.routing = s32[8,2]{1,0:T(8,128)} copy(s32[8,2]{0,1:T(2,128)} %param.8) | data formatting | bytes 128 | tf_op args[1]
  2.0 1.3 %reshape.24.mag = f32[1,3584]{1,0:T(1,128)} reshape(f32[3584]{0:T(1024)} %param.12) | data formatting | bytes 28672 | tf_op jit(solution)/shard_map/reshape | solution.py:428
  3.3 108.8 %shard_map.102 = (bf16[2,128,3584]{2,1,0:T(8,128)(2,1)}, f32[32,2048]{1,0:T(8,128)}, f32[32,3584]{1,0:T(8,128)}, f32[1,3584]{1,0:T(1,128)}) custom-call(bf16[2,8,16,2048]{3,2,1,0:T(8,128)(2,1)} %bitcast.5, s32[8,2]{1,0:T(8,128)} %copy.11.routing, bf16[2048,3584]{1,0:T(8,128)(2,1)} %w_hbm.1, bf16[32,2048]{1,0:T(8,128)(2,1)} %down.1, bf16[32,3584]{1,0:T(8,128)(2,1)} %up.1, ...), custom_call_target="tpu_custom_call" | custom-call | tf_op jit(solution)/shard_map/pallas_call | solution.py:370
  112.2 1.4 %reduce = f32[3584]{0:T(1024)} reduce(f32[1,3584]{1,0:T(1,128)} %get-tuple-element.11, f32[]{:T(128)} %constant), dimensions={0}, to_apply=%get-tuple-element.11.reduce_sub_computation | reduce | bytes 28676 | tf_op jit(solution)/shard_map/pallas_call | solution.py:370
  113.5 0.0 copy-start.1
  113.5 0.0 copy-start
  113.5 2.9 %copy.15 = bf16[256,3584]{1,0:T(8,128)(2,1)} copy(bf16[256,3584]{1,0:T(8,128)(2,1)} %bitcast.3) | data formatting | bytes 3670016
  116.4 0.0 copy-done.1
  116.4 0.7 copy.16
  117.1 0.0 copy-done
  117.1 0.8 copy.17
Async XLA Ops:
  113.5 2.9 %copy-start.1 = (f32[32,2048]{1,0:T(8,128)S(1)}, f32[32,2048]{1,0:T(8,128)}, u32[]{:S(2)}) copy-start(f32[32,2048]{1,0:T(8,128)} %get-tuple-element.17) | copy-start | bytes 786436
  113.5 3.6 %copy-start = (f32[32,3584]{1,0:T(8,128)S(1)}, f32[32,3584]{1,0:T(8,128)}, u32[]{:S(2)}) copy-start(f32[32,3584]{1,0:T(8,128)} %get-tuple-element.18) | copy-start | bytes 1376260

commit v2 on v1

--- a/solution.py
+++ b/solution.py
@@ -11,7 +11,10 @@
 BLK = 128
 ROWS = 16
 CHUNKS = BLK // ROWS
-AHEAD = 3
+HALVES = 2
+UNITS = CHUNKS * HALVES
+AHEAD = 2
+LAG = 2
 LANES = 128
 MESH = pl.DeviceIdType.MESH
 F32 = jnp.float32
@@ -40,8 +43,10 @@
     tok_in, routing, w_hbm, down, up, mag, cot,
     out, ga_out, gb_out, gm_out,
     w, raw, tok, part, near, pair, far, downp, sq, sq_near, sq_far, factor, norm, sg,
-    rp, rp_in, rgt, rg, proj_down, gm_acc, gb_part, gb_near, gb_sum, gb_far, gm_part, gm_in,
+    rp, rp_in, rgt, rg, proj_down, gm_acc, gb_part, gb_near, gb_sum, gb_far, gb_all, gm_part, gm_in,
+    d_part, d_near, d_pair, d_far,
     w_sem, s0_send, s0_recv, st_send, st_recv, nr_send, nr_recv, fr_send, fr_recv, ms_send, ms_recv,
+    dn_send, dn_recv, df_send, df_recv,
 ):
     dp, tp, width, cols, rank, tile, tps = cfg
     bits = dp.bit_length() - 1
@@ -71,14 +76,24 @@
         at = pl.ds(pl.multiple_of(n * tile, tile), tile)
         return pltpu.make_async_copy(w_hbm.at[:, at], w.at[:, at], w_sem.at[n])
 
-    def first(c):
-        return copy(tok_in.at[:, c], raw.at[c], s0_send.at[c], s0_recv.at[c], to_dp(0))
-
-    def stage(k, c, owner):
+    half = width // HALVES
+
+    def lanes(u):
+        return pl.ds(pl.multiple_of(u % HALVES * half, half), half)
+
+    def first(u):
+        c = u // HALVES
+        return copy(
+            tok_in.at[:, c, :, lanes(u)], raw.at[c, :, :, lanes(u)],
+            s0_send.at[u], s0_recv.at[u], to_dp(0),
+        )
+
+    def stage(k, u, owner):
         size = 1 << k
         base = mirrored(owner, bits) // size * size
-        here = tok.at[c, pl.ds(pl.multiple_of(base * ROWS, ROWS), size * ROWS)]
-        return copy(here, here, st_send.at[k - 1, c], st_recv.at[k - 1, c], to_dp(k))
+        rows = pl.ds(pl.multiple_of(base * ROWS, ROWS), size * ROWS)
+        here = tok.at[u // HALVES, rows, lanes(u)]
+        return copy(here, here, st_send.at[k - 1, u], st_recv.at[k - 1, u], to_dp(k))
 
     def near_copy(c):
         start = (1 - core) * 2
@@ -87,12 +102,19 @@
     def far_copy(c):
         return copy(pair.at[c], far.at[c], fr_send.at[c], fr_recv.at[c], far_id)
 
+    def down_near(c):
+        start = (1 - core) * 2
+        return copy(d_part.at[c, :, pl.ds(start, 2)], d_near.at[c], dn_send.at[c], dn_recv.at[c], near_id)
+
+    def down_far(c):
+        return copy(d_pair.at[c], d_far.at[c], df_send.at[c], df_recv.at[c], far_id)
+
     def small(n, src, dst, target):
         return copy(src, dst, ms_send.at[n], ms_recv.at[n], target)
 
     sq1 = small(0, sq, sq_near, near_id)
     sq2 = small(1, sq_near, sq_far, far_id)
-    rp_hops = [small(2 + k, rp.at[k], rp_in.at[k], to_dp(k)) for k in range(bits)]
+    rp_hops = [small(2 + k, rp.at[k], rp_in.at[k], to_dp(bits - 1 - k)) for k in range(bits)]
     n0 = 2 + bits
     rg1 = small(n0, rgt.at[t], rgt.at[t], near_id)
     rg1_in = small(n0, rgt.at[t_near], rgt.at[t_near], near_id)
@@ -144,7 +166,7 @@
         def body(at):
             square = sq_near[:, at] + sq_far[:, at]
             size = jnp.maximum(jnp.sqrt(square), 0.5)
-            ratio = mag[:, at] / size
+            ratio = mag[at].reshape(1, tile) / size
             norm[:, at] = size
             factor[:, at] = ratio
             for g in range(per):
@@ -167,9 +189,7 @@
                 + far[c, :, :, at].astype(F32)
             ).reshape(high, wide)
 
-        small_down = total(pl.ds(cols, LANES), LANES).astype(BF16)
-        proj_down[:, rows, :] = small_down.reshape(per, ROWS, LANES)
-        lhs = small_down[:, :rank]
+        lhs = proj_down[:, rows, :].reshape(high, LANES)[:, :rank]
 
         def body(at):
             pre = total(at, tile) + scale * jnp.dot(lhs, up[:, at], preferred_element_type=F32)
@@ -182,51 +202,55 @@
     def when(condition, action):
         pl.when(condition)(action)
 
-    steps = CHUNKS + bits + 1
-
-    @pl.loop(0, steps)
-    def _(i):
-        when(i + AHEAD < CHUNKS, lambda: first(i + AHEAD).start())
-
-        @pl.when(i < CHUNKS)
-        def _():
-            first(i).wait_recv()
+    grad_at = norm_last + 2
+    gap = max(1, (UNITS + 1 - grad_at) // bits)
+    parts = -(-tiles // 2)
+
+    @pl.loop(0, UNITS + LAG * (bits - 1) + 2)
+    def _(u):
+        when(u + AHEAD < UNITS, lambda: first(u + AHEAD).start())
+
+        @pl.when(u < UNITS)
+        def _():
+            first(u).wait_recv()
+            c = u // HALVES
+            at = lanes(u)
             own_at = pl.ds(pl.multiple_of(mirrored(d, bits) * ROWS, ROWS), ROWS)
             pair_at = pl.ds(pl.multiple_of(mirrored(hops[0], bits) * ROWS, ROWS), ROWS)
-            tok[i, own_at] = jnp.where(own_live, tok_in[0, i], raw[i, 1])
-            tok[i, pair_at] = jnp.where(pair_live, raw[i, 0], tok_in[1, i])
-            stage(1, i, d).start()
+            tok[c, own_at, at] = jnp.where(own_live, tok_in[0, c, :, at], raw[c, 1, :, at])
+            tok[c, pair_at, at] = jnp.where(pair_live, raw[c, 0, :, at], tok_in[1, c, :, at])
+            stage(1, u, d).start()
 
         for k in range(1, bits):
-            j = i - k
-
-            @pl.when((j >= 0) & (j < CHUNKS))
+            v = u - LAG * k
+
+            @pl.when((v >= 0) & (v < UNITS))
             def _():
-                stage(k, j, hops[k]).wait_recv()
+                stage(k, v, hops[k]).wait_recv()
                 if k < bits - 1:
-                    stage(k + 1, j, d).start()
-
-        @pl.when(i <= norm_last)
+                    stage(k + 1, v, d).start()
+
+        @pl.when(u <= norm_last)
         def _():
             for e in range(tps):
-                n = i * tps + e
+                n = u * tps + e
                 when(n < tiles, lambda: norm_tile(n))
 
-        when(i == norm_last, lambda: sq1.start())
-
-        @pl.when(i == norm_last + 1)
+        when(u == norm_last, lambda: sq1.start())
+
+        @pl.when(u == norm_last + 1)
         def _():
             sq1.wait()
             sq_near[...] = sq_near[...] + sq[...]
             sq2.start()
 
-        @pl.when(i == norm_last + 2)
+        @pl.when(u == grad_at)
         def _():
             sq2.wait()
             gradient()
 
         for k in range(bits):
-            @pl.when(i == norm_last + 3 + k)
+            @pl.when(u == grad_at + gap * (k + 1))
             def _():
                 rp_hops[k].wait()
                 merged = rp[k] + rp_in[k]
@@ -237,51 +261,105 @@
                     rgt[t] = merged.astype(BF16)
                     rg1.start()
 
-        @pl.when(i == norm_last + 3 + bits)
+        @pl.when(u == grad_at + gap * bits + 1)
         def _():
             rg1.wait_send()
             rg1_in.wait_recv()
             rg2.start()
 
-        j_near = i - bits
-
-        @pl.when((j_near >= 0) & (j_near < CHUNKS))
-        def _():
-            near_copy(j_near).wait_recv()
+        m = u - LAG * (bits - 1) - 1
+        j = m // 2
+        even = m % 2 == 0
+
+        @pl.when((m >= 2) & even)
+        def _():
+            c = j - 1
+            near_copy(c).wait_recv()
             other = core * 2 + 1 - side
 
             def body(at):
-                pair[j_near, :, :, at] = (
-                    part[j_near, :, other, :, at].astype(F32)
-                    + near[j_near, :, 1 - side, :, at].astype(F32)
+                pair[c, :, :, at] = (
+                    part[c, :, other, :, at].astype(F32)
+                    + near[c, :, 1 - side, :, at].astype(F32)
                 ).astype(BF16)
 
             each_tile(body)
-            body(pl.ds(cols, LANES))
-            far_copy(j_near).start()
-
-        j_mat = i - (bits - 1)
-
-        @pl.when((j_mat >= 0) & (j_mat < CHUNKS))
-        def _():
-            lhs = tok.at[j_mat]
-
-            def body(at):
-                prod = jnp.dot(lhs[...], w[:, at], preferred_element_type=F32)
-                part[j_mat, :, :, :, at] = prod.astype(BF16).reshape(per, tp, ROWS, tile)
-
-            each_tile(body)
-            part[j_mat, :, :, :, cols:] = (
-                dots(lhs[...], downp[...], 1, 1).astype(BF16).reshape(per, tp, ROWS, LANES)
-            )
-            near_copy(j_mat).start()
-
-        j_far = i - bits - 1
-
-        @pl.when((j_far >= 0) & (j_far < CHUNKS - 1))
-        def _():
-            far_copy(j_far).wait_recv()
-            epilogue(j_far)
+            far_copy(c).start()
+
+        @pl.when((m >= 0) & even & (j < CHUNKS))
+        def _():
+            d_part[j] = dots(tok[j], downp[...], 1, 1).astype(BF16).reshape(per, tp, ROWS, LANES)
+            down_near(j).start()
+
+        @pl.when((m >= 0) & (j < CHUNKS))
+        def _():
+            lhs = tok.at[j]
+            begin = (m % 2) * parts
+
+            @pl.loop(0, parts)
+            def _(e):
+                n = begin + e
+
+                @pl.when(n < tiles)
+                def _():
+                    at = pl.ds(pl.multiple_of(n * tile, tile), tile)
+                    prod = jnp.dot(lhs[...], w[:, at], preferred_element_type=F32)
+                    part[j, :, :, :, at] = prod.astype(BF16).reshape(per, tp, ROWS, tile)
+
+        @pl.when((m >= 0) & (m % 2 == 1) & (j < CHUNKS))
+        def _():
+            near_copy(j).start()
+            down_near(j).wait_recv()
+            d_pair[j] = (
+                d_part[j, :, core * 2 + 1 - side].astype(F32) + d_near[j, :, 1 - side].astype(F32)
+            ).astype(BF16)
+            down_far(j).start()
+
+        @pl.when((m >= 2) & even)
+        def _():
+            c = j - 1
+            down_far(c).wait_recv()
+            rows = pl.ds(pl.multiple_of(c * ROWS, ROWS), ROWS)
+            proj_down[:, rows, :] = (
+                d_part[c, :, core * 2 + side].astype(F32)
+                + d_near[c, :, side].astype(F32)
+                + d_far[c].astype(F32)
+            ).astype(BF16)
+
+        @pl.when((m >= 5) & (m % 2 == 1))
+        def _():
+            c = (m - 5) // 2
+            far_copy(c).wait_recv()
+            epilogue(c)
+
+    n1 = n0 + 2
+    share = rank // 2
+    gb1 = small(n1, gb_part.at[1 - core], gb_near, near_id)
+    gb2 = small(n1 + 1, gb_sum, gb_far, far_id)
+    gb3 = small(n1 + 4, gb_all.at[core], gb_all.at[core], near_id)
+    gb3_in = small(n1 + 4, gb_all.at[1 - core], gb_all.at[1 - core], near_id)
+    gm1 = small(n1 + 2, gm_part.at[0], gm_in.at[0], near_id)
+    gm2 = small(n1 + 3, gm_part.at[1], gm_in.at[1], far_id)
+    live = proj_down[...].reshape(per * BLK, LANES)[:, :rank]
+
+    def ends(at):
+        gb_part[:, :, at] = (
+            scale * dots(live, sg[:, :, at].reshape(per * BLK, tile), 0, 0)
+        ).astype(BF16).reshape(2, share, tile)
+
+    each_tile(ends)
+    gb1.start()
+
+    far_copy(CHUNKS - 2).wait_recv()
+    epilogue(CHUNKS - 2)
+
+    gb1.wait()
+
+    def sums(at):
+        gb_sum[:, at] = (gb_part[core, :, at].astype(F32) + gb_near[:, at].astype(F32)).astype(BF16)
+
+    each_tile(sums)
+    gb2.start()
 
     rg2.wait_send()
     rg2_in.wait_recv()
@@ -289,9 +367,7 @@
         turned = rgt[s].astype(F32).T.astype(BF16)
         spot = s % 2 * 2 + s // 2
         for g in range(per):
-            for c in range(CHUNKS):
-                low = g * BLK + c * ROWS
-                rg[c, g, spot] = turned[low:low + ROWS]
+            rg[:, g, spot] = turned[g * BLK:(g + 1) * BLK].reshape(CHUNKS, ROWS, rank)
 
     wide = min(512, width)
 
@@ -307,50 +383,41 @@
     far_copy(CHUNKS - 1).wait_recv()
     epilogue(CHUNKS - 1)
 
-    n1 = n0 + 2
-    gb1 = small(n1, gb_part, gb_near, near_id)
-    gb2 = small(n1 + 1, gb_sum, gb_far, far_id)
-    gm1 = small(n1 + 2, gm_part.at[0], gm_in.at[0], near_id)
-    gm2 = small(n1 + 3, gm_part.at[1], gm_in.at[1], far_id)
-    live = proj_down[...].reshape(per * BLK, LANES)[:, :rank]
-
-    def ends(at):
-        gb_part[:, at] = (
-            scale * dots(live, sg[:, :, at].reshape(per * BLK, tile), 0, 0)
-        ).astype(BF16)
+    def shares(at):
         gm_part[0, :, at] = (
             jnp.sum(gm_acc[:, at], axis=0, keepdims=True) / norm[:, at] * inverse
         )
 
-    each_tile(ends)
+    each_tile(shares)
     gm1.start()
-    gb1.start()
     gm1.wait()
     gm_part[1] = gm_part[0] + gm_in[0]
     gm2.start()
-    gb1.wait()
-
-    def sums(at):
-        gb_sum[:, at] = (gb_part[:, at].astype(F32) + gb_near[:, at].astype(F32)).astype(BF16)
-
-    each_tile(sums)
-    gb2.start()
+    gb2.wait()
+
+    def last(at):
+        gb_all[core, :, at] = gb_sum[:, at].astype(F32) + gb_far[:, at].astype(F32)
+
+    each_tile(last)
+    gb3.start()
     gm2.wait()
-    gm_out[...] = gm_part[1] + gm_in[1]
-    gb2.wait()
-
-    def last(at):
-        gb_out[:, at] = gb_sum[:, at].astype(F32) + gb_far[:, at].astype(F32)
-
-    each_tile(last)
+    gm_out[...] = (gm_part[1] + gm_in[1]).reshape(cols)
+    gb3.wait_send()
+    gb3_in.wait_recv()
+    gb_out[...] = gb_all[...].reshape(rank, cols)
+
+    @pl.loop(0, UNITS)
+    def _(u):
+        first(u).wait_send()
+        for k in range(1, bits):
+            stage(k, u, d).wait_send()
 
     @pl.loop(0, CHUNKS)
     def _(c):
-        first(c).wait_send()
-        for k in range(1, bits):
-            stage(k, c, d).wait_send()
         near_copy(c).wait_send()
         far_copy(c).wait_send()
+        down_near(c).wait_send()
+        down_far(c).wait_send()
 
 
 def body(dp, tp, tokens, routing, weight, down, up, mag, cot):
@@ -360,20 +427,20 @@
     bits = dp.bit_length() - 1
     tile = next(size for size in (512, 256, 128) if cols % size == 0)
     tiles = cols // tile
-    tps = -(-tiles // bits)
+    tps = -(-tiles // (bits + 1))
     cfg = (dp, tp, width, cols, rank, tile, tps)
-    ext = cols + LANES
+    ext = cols
     vmem = pl.BlockSpec(memory_space=pltpu.VMEM)
     dma = pltpu.SemaphoreType.DMA
     mine = per * BLK
-    misc = bits + 8
+    misc = bits + 9
     out, ga, gb, gm = pl.pallas_call(
         functools.partial(kernel, cfg),
         out_shape=(
             jax.ShapeDtypeStruct((per, BLK, cols), BF16),
             jax.ShapeDtypeStruct((rank, width), F32),
             jax.ShapeDtypeStruct((rank, cols), F32),
-            jax.ShapeDtypeStruct((1, cols), F32),
+            jax.ShapeDtypeStruct((cols,), F32),
         ),
         in_specs=[
             vmem,
@@ -403,18 +470,25 @@
             pltpu.VMEM((CHUNKS, per, tp, ROWS, rank), BF16),
             pltpu.VMEM((per, BLK, LANES), BF16),
             pltpu.VMEM((8, cols), F32),
-            pltpu.VMEM((rank, cols), BF16),
-            pltpu.VMEM((rank, cols), BF16),
-            pltpu.VMEM((rank, cols), BF16),
-            pltpu.VMEM((rank, cols), BF16),
+            pltpu.VMEM((2, rank // 2, cols), BF16),
+            pltpu.VMEM((rank // 2, cols), BF16),
+            pltpu.VMEM((rank // 2, cols), BF16),
+            pltpu.VMEM((rank // 2, cols), BF16),
+            pltpu.VMEM((2, rank // 2, cols), F32),
             pltpu.VMEM((2, 1, cols), F32),
             pltpu.VMEM((2, 1, cols), F32),
+            pltpu.VMEM((CHUNKS, per, tp, ROWS, LANES), BF16),
+            pltpu.VMEM((CHUNKS, per, 2, ROWS, LANES), BF16),
+            pltpu.VMEM((CHUNKS, per, ROWS, LANES), BF16),
+            pltpu.VMEM((CHUNKS, per, ROWS, LANES), BF16),
             dma((tiles,)),
-            dma((CHUNKS,)), dma((CHUNKS,)),
-            dma((bits - 1, CHUNKS)), dma((bits - 1, CHUNKS)),
+            dma((UNITS,)), dma((UNITS,)),
+            dma((bits - 1, UNITS)), dma((bits - 1, UNITS)),
             dma((CHUNKS,)), dma((CHUNKS,)),
             dma((CHUNKS,)), dma((CHUNKS,)),
             dma((misc,)), dma((misc,)),
+            dma((CHUNKS,)), dma((CHUNKS,)),
+            dma((CHUNKS,)), dma((CHUNKS,)),
         ],
         compiler_params=pltpu.CompilerParams(
             collective_id=0, has_side_effects=True, vmem_limit_bytes=67043328
@@ -425,10 +499,10 @@
         weight,
         down,
         up,
-        mag.reshape(1, cols),
+        mag,
         cot.reshape(per, BLK, cols),
     )
-    return out.reshape(mine, cols), ga, gb, gm.reshape(cols)
+    return out.reshape(mine, cols), ga, gb, gm
 
 
 def solution(mesh):

time: 118 us -> 105 us (0.89)
  Pallas kernels: 109 us -> 97.4 us
  other arithmetic: 1.36 us -> 0 us
    pallas_call x1, Pallas kernels: 109 us -> 97.4 us  [body(): pl.pallas_call(functools.partial(kernel, cfg), out_shape=(jax.ShapeDtypeS...]
    pallas_call x1 -> x0, other arithmetic: 1.36 us -> none  [body(): pl.pallas_call(functools.partial(kernel, cfg), out_shape=(jax.ShapeDtypeS...]
    reshape x1 -> x0, local copies, waits for them, and re-layouts: 1.33 us -> none  [body(): mag.reshape(1, cols)]
    unnamed x8 -> x11, local copies, waits for them, and re-layouts: 5.74 us -> 6.35 us
where the time goes in v2:
time: 105 us; the launch traced here: 104 us
  Pallas kernels  97.4 us (93%)
  local copies, waits for them, and re-layouts  6.35 us (6%)
    pallas_call x1, Pallas kernels, body(): pl.pallas_call(functools.partial(kernel, cfg), out_shape=(jax.ShapeDtypeS...  97.4 us
    unnamed x11, local copies, waits for them, and re-layouts  6.35 us

profile of v2, /device:TPU:0, one launch (start us, length us, event | category | flops | bytes accessed | tf_op | source)
XLA Modules:
  0.0 104.4 jit_solution(17511962856952761503)
XLA Ops:
  0.6 1.3 %copy.11.routing = s32[8,2]{1,0:T(8,128)} copy(s32[8,2]{0,1:T(2,128)} %param.8) | data formatting | bytes 128 | tf_op args[1]
  2.0 97.4 %shard_map.102 = (bf16[2,128,3584]{2,1,0:T(8,128)(2,1)}, f32[32,2048]{1,0:T(8,128)}, f32[32,3584]{1,0:T(8,128)}, f32[3584]{0:T(1024)}) custom-call(bf16[2,8,16,2048]{3,2,1,0:T(8,128)(2,1)} %bitcast.5, s32[8,2]{1,0:T(8,128)} %copy.11.routing, bf16[2048,3584]{1,0:T(8,128)(2,1)} %w_hbm.1, bf16[32,2048]{1,0:T(8,128)(2,1)} %down.1, bf16[32,3584]{1,0:T(8,128)(2,1)} %up.1, ...), custom_call_target="tpu_custom_call" | custom-call | tf_op jit(solution)/shard_map/pallas_call | solution.py:437
  99.3 0.0 copy-start.1
  99.4 0.0 copy-start
  99.4 0.0 copy-start.2
  99.4 2.9 %copy.16 = bf16[256,3584]{1,0:T(8,128)(2,1)} copy(bf16[256,3584]{1,0:T(8,128)(2,1)} %bitcast.4) | data formatting | bytes 3670016
  102.3 0.0 copy-done.1
  102.3 0.7 copy.17
  103.0 0.0 copy-done
  103.0 0.8 copy.18
  103.8 0.0 copy-done.2
  103.8 0.6 copy.19
Async XLA Ops:
  99.3 2.9 %copy-start.1 = (f32[32,2048]{1,0:T(8,128)S(1)}, f32[32,2048]{1,0:T(8,128)}, u32[]{:S(2)}) copy-start(f32[32,2048]{1,0:T(8,128)} %get-tuple-element.17) | copy-start | bytes 786436
  99.4 3.6 %copy-start = (f32[32,3584]{1,0:T(8,128)S(1)}, f32[32,3584]{1,0:T(8,128)}, u32[]{:S(2)}) copy-start(f32[32,3584]{1,0:T(8,128)} %get-tuple-element.18) | copy-start | bytes 1376260
  99.4 4.4 %copy-start.2 = (f32[3584]{0:T(1024)S(1)}, f32[3584]{0:T(1024)}, u32[]{:S(2)}) copy-start(f32[3584]{0:T(1024)} %get-tuple-element.19) | copy-start | bytes 43012
